TPU v7x, 32 devices: a whole 2x2x4 slice. The times are simulated.
32 devices in a mesh: task: 8 (over z, y), occ: 4 (over x, core).
Axes of the slice: x: 2, y: 2, z: 4, core: 2. Of those that a mesh axis runs over, the one named last changes fastest.
Arguments:
- ao_tiles: bfloat16 [1280, 8, 32, 128], P('task'), may hold values from -6 to 6
- mo_coeffs: bfloat16 [1536, 200], P(None, 'occ'), may hold values from -0.5 to 0.5
- mu_blocks: int32 [1280], P('task'), may hold values from 0 to 191
- nu_blocks: int32 [1280], P('task'), may hold values from 0 to 47
- tile_live: int32 [1280], P('task'), may hold values 0 or 1
- batch_target: int32 [160], P('task'), may hold values from 0 to 2
- batch_count: int32 [8], P('task'), may hold values from 1 to 20
Outputs:
- half_mo: float32 [200, 200, 1024], P('occ', None, 'task')
Inputs may be any that keep to these rules, and one draw needn't show every extreme that they name: `batch_target`: the batch's kl block is the block owned by task index (own index + value) mod 8. `batch_count`: batches at or after this count in a list are not part of the work.
All inputs are finite; a program needn't handle non-finite values. No bound on the sum of `tile_live` on one device may be relied on, other than what follows from the above.
Results may differ from a plain program's by a relative error of at most 0.0029.
Values may be sent and summed in bfloat16 or wider, within the bound.
A program may use at most 128 MiB of HBM per device.

v0:
```python
from functools import partial

import jax
import jax.numpy as jnp
from jax import lax
from jax.experimental import pallas as pl
from jax.experimental.pallas import tpu as pltpu
from jax.sharding import PartitionSpec as P

SPREAD = 3
GROUP = 8
F32 = jnp.float32
BF16 = jnp.bfloat16


def plan_kernel(live_ref, target_ref, count_ref, slots_ref, filled_ref):
    per_batch = live_ref.shape[0] // target_ref.shape[0]
    room = live_ref.shape[0] + GROUP
    for s in range(SPREAD):
        filled_ref[s] = 0

    def take_batch(batch, carry):
        target = target_ref[batch]
        at = filled_ref[target]
        for q in range(per_batch):
            tile = batch * per_batch + q
            slots_ref[target * room + at] = tile
            at = at + live_ref[tile]
        filled_ref[target] = at
        return carry

    lax.fori_loop(0, count_ref[0], take_batch, 0)
    for s in range(SPREAD):
        end = filled_ref[s]
        for q in range(GROUP):
            slots_ref[s * room + end + q] = 0


def make_plan(tile_live, batch_target, batch_count):
    smem = pl.BlockSpec(memory_space=pltpu.SMEM)
    room = tile_live.shape[0] + GROUP
    return pl.pallas_call(
        plan_kernel,
        out_shape=(
            jax.ShapeDtypeStruct((SPREAD * room,), jnp.int32),
            jax.ShapeDtypeStruct((SPREAD,), jnp.int32),
        ),
        in_specs=[smem] * 3,
        out_specs=(smem, smem),
        name="plan",
    )(tile_live, batch_target, batch_count)


def contract_kernel(targets, room, slots_ref, filled_ref, mu_ref, nu_ref, tiles, *refs):
    coeff_i, coeff_all, pick, own, interleave, unit = refs[:6]
    outs = refs[6 : 6 + len(targets)]
    held, turned, quarter, total, landed = refs[6 + len(targets) :]
    _, mu_width, nu_width, kl = tiles.shape
    occ = total.shape[0]
    depth = GROUP * mu_width
    across = (((1,), (1,)), ((), ()))

    def fetch(target, group, slot):
        return [
            pltpu.make_async_copy(
                tiles.at[slots_ref[target * room + group * GROUP + b]], held.at[slot, b], landed.at[slot]
            )
            for b in range(GROUP)
        ]

    def visit(target, groups, group, slot):
        for copy in fetch(target, group, slot):
            copy.wait()

        @pl.when(group + 1 < groups)
        def _():
            for copy in fetch(target, group + 1, 1 - slot):
                copy.start()

        for b in range(GROUP):
            for m in range(mu_width):
                turned[pl.ds(b * mu_width + m, nu_width, stride=depth), :] = held[slot, b, m].astype(F32)

        mus, nus = [], []
        for b in range(GROUP):
            place = group * GROUP + b
            tile = slots_ref[target * room + place]
            mus.append(coeff_i[mu_ref[tile]])
            rows = coeff_all[pl.ds(pl.multiple_of(nu_ref[tile] * nu_width, nu_width), nu_width), :]
            nus.append(rows.astype(F32) * jnp.where(place < filled_ref[target], 1.0, 0.0))
        mu_rows = jnp.concatenate(mus, axis=0).astype(BF16)
        nu_rows = jnp.concatenate(nus, axis=0).astype(BF16)
        left = lax.dot_general(pick[...], mu_rows, across, preferred_element_type=F32)
        left = (left * own[...]).astype(BF16)
        mixed = jnp.dot(interleave[...], nu_rows, preferred_element_type=F32).astype(BF16)
        right = lax.dot_general(unit[...], mixed, across, preferred_element_type=F32).astype(BF16)

        for p in range(nu_width // 2):
            even, later = 2 * p * depth, (2 * p + 1) * depth
            pair = jnp.concatenate(
                [turned[even : even + depth, :], turned[later : later + depth, :]], axis=1
            ).astype(BF16)
            got = jnp.dot(left, pair, preferred_element_type=F32).reshape(occ, GROUP, 2 * kl)
            got = jnp.concatenate([got[:, :, :kl], got[:, :, kl:]], axis=1)
            quarter[:, 2 * p * GROUP : (2 * p + 2) * GROUP, :] = got.astype(BF16)

        for h in range(occ // 2):
            both = jnp.concatenate([quarter[2 * h], quarter[2 * h + 1]], axis=1)
            got = jnp.dot(right, both, preferred_element_type=F32)
            total[2 * h] += got[:, :kl]
            total[2 * h + 1] += got[:, kl:]
        if occ % 2:
            total[occ - 1] += jnp.dot(right, quarter[occ - 1], preferred_element_type=F32)
        return 1 - slot

    for target, out in zip(targets, outs):
        groups = lax.div(filled_ref[target] + (GROUP - 1), GROUP)
        total[...] = jnp.zeros_like(total)

        @pl.when(groups > 0)
        def _(target=target):
            for copy in fetch(target, 0, 0):
                copy.start()

        lax.fori_loop(0, groups, lambda g, slot, t=target, n=groups: visit(t, n, g, slot), jnp.int32(0))
        out[...] = total[...].astype(out.dtype)


def contract(targets, dtype, start, occ, ao_tiles, coeff_i, coeff_all, plan, mu_blocks, nu_blocks):
    slots, filled = plan
    count, mu_width, nu_width, kl = ao_tiles.shape
    all_occ = coeff_all.shape[1]
    local_occ = coeff_i.shape[2]
    room = count + GROUP
    depth, width = GROUP * mu_width, GROUP * nu_width

    def eq(rows, columns):
        return rows[:, None] == columns[None, :]

    out_rows = jnp.arange(occ * GROUP)
    pick = eq(out_rows // GROUP + start, jnp.arange(local_occ)).astype(BF16)
    own = eq(out_rows % GROUP, jnp.arange(depth) // mu_width).astype(F32)
    mixed_rows = jnp.arange(width)
    interleave = eq(mixed_rows % GROUP * nu_width + mixed_rows // GROUP, mixed_rows).astype(BF16)
    unit = eq(jnp.arange(all_occ), jnp.arange(all_occ)).astype(BF16)
    shared = [coeff_i, coeff_all, pick, own, interleave, unit]
    share = occ * len(targets) * max(1, count // GROUP // SPREAD)
    outs = [jax.ShapeDtypeStruct((occ, all_occ, kl), dtype) for _ in targets]
    return pl.pallas_call(
        partial(contract_kernel, targets, room),
        out_shape=outs,
        in_specs=[pl.BlockSpec(memory_space=pltpu.SMEM)] * 4
        + [pl.BlockSpec(memory_space=pl.ANY)]
        + [pl.BlockSpec(memory_space=pltpu.VMEM)] * len(shared),
        out_specs=[pl.BlockSpec(memory_space=pltpu.VMEM) for _ in targets],
        scratch_shapes=[
            pltpu.VMEM((2, GROUP, mu_width, nu_width, kl), BF16),
            pltpu.VMEM((nu_width * depth, kl), F32),
            pltpu.VMEM((occ, width, kl), BF16),
            pltpu.VMEM((occ, all_occ, kl), F32),
            pltpu.SemaphoreType.DMA((2,)),
        ],
        compiler_params=pltpu.CompilerParams(vmem_limit_bytes=56 * 1024 * 1024),
        cost_estimate=pl.CostEstimate(
            flops=4 * share * all_occ * width * kl, bytes_accessed=share * all_occ * kl, transcendentals=0
        ),
        name="contract",
    )(slots, filled, mu_blocks, nu_blocks, ao_tiles, *shared)


def local(ao_tiles, mo_coeffs, mu_blocks, nu_blocks, tile_live, batch_target, batch_count):
    mu_width = ao_tiles.shape[1]
    local_occ = mo_coeffs.shape[1]
    plan = make_plan(tile_live, batch_target, batch_count)
    coeff_all = lax.all_gather(mo_coeffs, "occ", axis=1, tiled=True)
    coeff_i = mo_coeffs.astype(F32).reshape(-1, mu_width, local_occ)
    tasks = lax.axis_size("task")
    swap = [(t, t ^ 1) for t in range(tasks)]
    ahead = [(t, (t + 2) % tasks) for t in range(tasks)]
    odd = lax.axis_index("task") % 2 == 1

    pieces = next(n for n in range(min(5, local_occ), 0, -1) if local_occ % n == 0)
    occ = local_occ // pieces
    work = (ao_tiles, coeff_i, coeff_all, plan, mu_blocks, nu_blocks)
    swapped, arrived = [], []
    for c in range(pieces):
        one, two = contract((1, 2), BF16, c * occ, occ, *work)
        other = lax.ppermute(one, "task", swap)
        send = jnp.where(odd, two, (two.astype(F32) + other.astype(F32)).astype(BF16))
        arrived.append(lax.ppermute(send, "task", ahead))
        swapped.append(other)
    (result,) = contract((0,), F32, 0, local_occ, *work)
    for c in range(pieces):
        part = lax.slice_in_dim(result, c * occ, (c + 1) * occ, axis=0)
        part = part + (arrived[c].astype(F32) + jnp.where(odd, swapped[c].astype(F32), 0.0))
        result = lax.dynamic_update_slice_in_dim(result, part, c * occ, axis=0)
    return result


def solution(mesh):
    in_specs = (
        P("task", None, None, None),
        P(None, "occ"),
        P("task"),
        P("task"),
        P("task"),
        P("task"),
        P("task"),
    )
    out_specs = P("occ", None, "task")
    return jax.shard_map(local, mesh=mesh, in_specs=in_specs, out_specs=out_specs, check_vma=False)
```

profile of v0, /device:TPU:4, one launch (start us, length us, event | category | flops | bytes accessed | tf_op | source)
XLA Modules:
  0.0 197.2 jit_solution(10304656499951310650)
XLA Ops:
  0.0 0.7 fusion.27.refs_5_
  1.3 2.0 %copy.12 = f32[1536,50]{1,0:T(8,128)} copy(bf16[1536,50]{0,1:T(8,128)(2,1)} %param.8) | data formatting | bytes 460800 | tf_op jit(solution)/shard_map/reshape | solution.py:176
  3.3 8.3 %all-gather = bf16[4,50,1536]{2,1,0:T(8,128)(2,1)S(1)} all-gather(bf16[1,50,1536]{2,1,0:T(8,128)(2,1)} %bitcast.17), channel_id=1, replica_groups=mesh['task'=8,'occ'=4] {'occ'}, dimensions={0}, use_global_device_ids=true | all-gather | bytes 768000 | tf_op jit(solution)/shard_map/all_gather | solution.py:175
  11.6 0.2 reshape.101
  11.8 1.2 copy.13
  13.0 0.8 fusion.25.refs_4_
  13.7 0.7 fusion.28.refs_2_
  14.4 0.7 compare_convert_fusion.1.refs_3_
  15.1 1.5 plan.1
  16.6 12.8 %contract.7 = (bf16[10,200,128]{2,1,0:T(8,128)(2,1)}, bf16[10,200,128]{2,1,0:T(8,128)(2,1)}) custom-call(s32[504]{0:T(512)} %get-tuple-element.17.slots_ref, s32[3]{0:T(128)} %get-tuple-element.18.filled_ref, s32[160]{0:T(256)} %mu_ref.11, s32[160]{0:T(256)} %nu_ref.11, bf16[160,8,32,128]{3,2,1,0:T(8,128)(2,1)} %tiles.11, f32[192,8,50]{2,1,0:T(8,128)} %bitcast.5, ...), custom_call_target="tpu_custom_call" | custom-call | flops 3145728000 | bytes 3072000 | tf_op jit(solution)/shard_map/contract/pallas_call | solution.py:149
  29.4 3.3 %collective-permute-start = (bf16[10,200,128]{2,1,0:T(8,128)(2,1)}, bf16[10,200,128]{2,1,0:T(8,128)(2,1)S(1)}, u32[]{:S(2)}, u32[]{:S(2)}) collective-permute-start(bf16[10,200,128]{2,1,0:T(8,128)(2,1)} %get-tuple-element.20), channel_id=1, source_target_pairs={{0,4},{4,0},{8,12},{12,8},{16,20},{20,16},{24,28},{28,24},{1,5},{5... | collective-permute-start | bytes 1536008 | tf_op jit(solution)/shard_map/ppermute | solution.py:188
  32.8 0.7 fusion.29.refs_2_
  33.5 12.8 %contract.8 = (bf16[10,200,128]{2,1,0:T(8,128)(2,1)}, bf16[10,200,128]{2,1,0:T(8,128)(2,1)}) custom-call(s32[504]{0:T(512)} %get-tuple-element.17.slots_ref, s32[3]{0:T(128)} %get-tuple-element.18.filled_ref, s32[160]{0:T(256)} %mu_ref.11, s32[160]{0:T(256)} %nu_ref.11, bf16[160,8,32,128]{3,2,1,0:T(8,128)(2,1)} %tiles.11, f32[192,8,50]{2,1,0:T(8,128)} %bitcast.6, ...), custom_call_target="tpu_custom_call" | custom-call | flops 3145728000 | bytes 3072000 | tf_op jit(solution)/shard_map/contract/pallas_call | solution.py:149
  46.3 2.8 %collective-permute-start.2 = (bf16[10,200,128]{2,1,0:T(8,128)(2,1)}, bf16[10,200,128]{2,1,0:T(8,128)(2,1)S(1)}, u32[]{:S(2)}, u32[]{:S(2)}) collective-permute-start(bf16[10,200,128]{2,1,0:T(8,128)(2,1)} %get-tuple-element.22), channel_id=1, source_target_pairs={{0,4},{4,0},{8,12},{12,8},{16,20},{20,16},{24,28},{28,24},{1,5},{5... | collective-permute-start | bytes 1536008 | tf_op jit(solution)/shard_map/ppermute | solution.py:188
  49.1 0.7 fusion.30.refs_2_
  49.8 12.8 %contract.9 = (bf16[10,200,128]{2,1,0:T(8,128)(2,1)}, bf16[10,200,128]{2,1,0:T(8,128)(2,1)}) custom-call(s32[504]{0:T(512)} %get-tuple-element.17.slots_ref, s32[3]{0:T(128)} %get-tuple-element.18.filled_ref, s32[160]{0:T(256)} %mu_ref.11, s32[160]{0:T(256)} %nu_ref.11, bf16[160,8,32,128]{3,2,1,0:T(8,128)(2,1)} %tiles.11, f32[192,8,50]{2,1,0:T(8,128)} %bitcast.7, ...), custom_call_target="tpu_custom_call" | custom-call | flops 3145728000 | bytes 3072000 | tf_op jit(solution)/shard_map/contract/pallas_call | solution.py:149
  62.6 2.8 %collective-permute-start.4 = (bf16[10,200,128]{2,1,0:T(8,128)(2,1)}, bf16[10,200,128]{2,1,0:T(8,128)(2,1)S(1)}, u32[]{:S(2)}, u32[]{:S(2)}) collective-permute-start(bf16[10,200,128]{2,1,0:T(8,128)(2,1)} %get-tuple-element.24), channel_id=1, source_target_pairs={{0,4},{4,0},{8,12},{12,8},{16,20},{20,16},{24,28},{28,24},{1,5},{5... | collective-permute-start | bytes 1536008 | tf_op jit(solution)/shard_map/ppermute | solution.py:188
  65.5 0.7 fusion.31.refs_2_
  66.1 12.8 %contract.10 = (bf16[10,200,128]{2,1,0:T(8,128)(2,1)}, bf16[10,200,128]{2,1,0:T(8,128)(2,1)}) custom-call(s32[504]{0:T(512)} %get-tuple-element.17.slots_ref, s32[3]{0:T(128)} %get-tuple-element.18.filled_ref, s32[160]{0:T(256)} %mu_ref.11, s32[160]{0:T(256)} %nu_ref.11, bf16[160,8,32,128]{3,2,1,0:T(8,128)(2,1)} %tiles.11, f32[192,8,50]{2,1,0:T(8,128)} %bitcast.8, ...), custom_call_target="tpu_custom_call" | custom-call | flops 3145728000 | bytes 3072000 | tf_op jit(solution)/shard_map/contract/pallas_call | solution.py:149
  79.0 2.8 %collective-permute-start.6 = (bf16[10,200,128]{2,1,0:T(8,128)(2,1)}, bf16[10,200,128]{2,1,0:T(8,128)(2,1)S(1)}, u32[]{:S(2)}, u32[]{:S(2)}) collective-permute-start(bf16[10,200,128]{2,1,0:T(8,128)(2,1)} %get-tuple-element.26), channel_id=1, source_target_pairs={{0,4},{4,0},{8,12},{12,8},{16,20},{20,16},{24,28},{28,24},{1,5},{5... | collective-permute-start | bytes 1536008 | tf_op jit(solution)/shard_map/ppermute | solution.py:188
  81.8 0.7 fusion.32.refs_2_
  82.5 12.8 %contract.11 = (bf16[10,200,128]{2,1,0:T(8,128)(2,1)}, bf16[10,200,128]{2,1,0:T(8,128)(2,1)}) custom-call(s32[504]{0:T(512)} %get-tuple-element.17.slots_ref, s32[3]{0:T(128)} %get-tuple-element.18.filled_ref, s32[160]{0:T(256)} %mu_ref.11, s32[160]{0:T(256)} %nu_ref.11, bf16[160,8,32,128]{3,2,1,0:T(8,128)(2,1)} %tiles.11, f32[192,8,50]{2,1,0:T(8,128)} %bitcast.9, ...), custom_call_target="tpu_custom_call" | custom-call | flops 3145728000 | bytes 3072000 | tf_op jit(solution)/shard_map/contract/pallas_call | solution.py:149
  95.3 2.8 %collective-permute-start.8 = (bf16[10,200,128]{2,1,0:T(8,128)(2,1)}, bf16[10,200,128]{2,1,0:T(8,128)(2,1)S(1)}, u32[]{:S(2)}, u32[]{:S(2)}) collective-permute-start(bf16[10,200,128]{2,1,0:T(8,128)(2,1)} %get-tuple-element.28), channel_id=1, source_target_pairs={{0,4},{4,0},{8,12},{12,8},{16,20},{20,16},{24,28},{28,24},{1,5},{5... | collective-permute-start | bytes 1536008 | tf_op jit(solution)/shard_map/ppermute | solution.py:188
  98.2 0.8 compare_convert_fusion.refs_3_
  99.0 0.8 fusion.26.refs_2_
  99.8 0.0 copy-start.2
  99.8 15.0 %contract.6 = f32[50,200,128]{2,1,0:T(8,128)} custom-call(s32[504]{0:T(512)} %get-tuple-element.17.slots_ref, s32[3]{0:T(128)} %get-tuple-element.18.filled_ref, s32[160]{0:T(256)} %mu_ref.11, s32[160]{0:T(256)} %nu_ref.11, bf16[160,8,32,128]{3,2,1,0:T(8,128)(2,1)} %tiles.11, f32[192,8,50]{2,1,0:T(8,128)} %bitcast.10, bf16[1536,200]{1,0:T(8,128)(2,1)} %bitcast.16, ...), custom_call_target="tpu_custom_call" | custom-call | flops 7864320000 | bytes 7680000 | tf_op jit(solution)/shard_map/contract/pallas_call | solution.py:149
  114.8 0.0 copy-start.3
  114.8 0.0 copy-start
  114.8 0.0 collective-permute-done
  114.8 0.0 copy-done.2
  114.8 0.2 fusion.24
  115.0 12.4 %collective-permute-start.1 = (bf16[10,200,128]{2,1,0:T(8,128)(2,1)S(1)}, bf16[10,200,128]{2,1,0:T(8,128)(2,1)S(1)}, u32[]{:S(2)}, u32[]{:S(2)}) collective-permute-start(bf16[10,200,128]{2,1,0:T(8,128)(2,1)S(1)} %fusion.24), channel_id=1, source_target_pairs={{0,8},{4,12},{8,16},{12,20},{16,24},{20,28},{24,0},{28,4},{1,9},{5... | collective-permute-start | bytes 1536008 | tf_op jit(solution)/shard_map/ppermute | solution.py:190
  127.4 0.0 collective-permute-done.2
  127.4 1.4 fusion.23
  128.8 0.2 collective-permute-start.3
  129.0 0.0 collective-permute-done.4
  129.0 1.4 fusion.22
  130.4 12.4 %collective-permute-start.5 = (bf16[10,200,128]{2,1,0:T(8,128)(2,1)S(1)}, bf16[10,200,128]{2,1,0:T(8,128)(2,1)S(1)}, u32[]{:S(2)}, u32[]{:S(2)}) collective-permute-start(bf16[10,200,128]{2,1,0:T(8,128)(2,1)S(1)} %fusion.22), channel_id=1, source_target_pairs={{0,8},{4,12},{8,16},{12,20},{16,24},{20,28},{24,0},{28,4},{1,9},{5... | collective-permute-start | bytes 1536008 | tf_op jit(solution)/shard_map/ppermute | solution.py:190
  142.9 0.0 collective-permute-done.6
  142.9 1.4 fusion.21
  144.3 0.2 collective-permute-start.7
  144.5 0.0 collective-permute-done.8
  144.5 0.0 copy-done.3
  144.5 0.2 fusion.20
  144.7 0.1 collective-permute-start.9
  144.8 6.6 %collective-permute-done.1 = bf16[10,200,128]{2,1,0:T(8,128)(2,1)S(1)} collective-permute-done((bf16[10,200,128]{2,1,0:T(8,128)(2,1)S(1)}, bf16[10,200,128]{2,1,0:T(8,128)(2,1)S(1)}, u32[]{:S(2)}, u32[]{:S(2)}) %collective-permute-start.1) | collective-permute-done | bytes 512032 | tf_op jit(solution)/shard_map/ppermute | solution.py:190
  151.3 0.0 copy-done
  151.3 0.4 fusion.3
  151.7 10.6 %collective-permute-done.3 = bf16[10,200,128]{2,1,0:T(8,128)(2,1)S(1)} collective-permute-done((bf16[10,200,128]{2,1,0:T(8,128)(2,1)S(1)}, bf16[10,200,128]{2,1,0:T(8,128)(2,1)S(1)}, u32[]{:S(2)}, u32[]{:S(2)}) %collective-permute-start.3) | collective-permute-done | bytes 512032 | tf_op jit(solution)/shard_map/ppermute | solution.py:190
  162.3 0.4 fusion.7
  162.7 10.6 %collective-permute-done.5 = bf16[10,200,128]{2,1,0:T(8,128)(2,1)S(1)} collective-permute-done((bf16[10,200,128]{2,1,0:T(8,128)(2,1)S(1)}, bf16[10,200,128]{2,1,0:T(8,128)(2,1)S(1)}, u32[]{:S(2)}, u32[]{:S(2)}) %collective-permute-start.5) | collective-permute-done | bytes 512032 | tf_op jit(solution)/shard_map/ppermute | solution.py:190
  173.3 0.4 fusion.11
  173.7 10.6 %collective-permute-done.7 = bf16[10,200,128]{2,1,0:T(8,128)(2,1)S(1)} collective-permute-done((bf16[10,200,128]{2,1,0:T(8,128)(2,1)S(1)}, bf16[10,200,128]{2,1,0:T(8,128)(2,1)S(1)}, u32[]{:S(2)}, u32[]{:S(2)}) %collective-permute-start.7) | collective-permute-done | bytes 512032 | tf_op jit(solution)/shard_map/ppermute | solution.py:190
  184.2 0.4 fusion.15
  184.6 0.0 copy-start.1
  184.6 10.2 %collective-permute-done.9 = bf16[10,200,128]{2,1,0:T(8,128)(2,1)S(1)} collective-permute-done((bf16[10,200,128]{2,1,0:T(8,128)(2,1)S(1)}, bf16[10,200,128]{2,1,0:T(8,128)(2,1)S(1)}, u32[]{:S(2)}, u32[]{:S(2)}) %collective-permute-start.9) | collective-permute-done | bytes 512032 | tf_op jit(solution)/shard_map/ppermute | solution.py:190
  194.9 0.0 copy-done.1
  194.9 2.4 %fusion.19 = f32[50,200,128]{2,1,0:T(8,128)} fusion(f32[50,200,128]{2,1,0:T(8,128)} %copy-done.1, bf16[10,200,128]{2,1,0:T(8,128)(2,1)S(1)} %collective-permute-done.8, bf16[10,200,128]{2,1,0:T(8,128)(2,1)S(1)} %collective-permute-done.9, pred[]{:T(512)S(6)} %eq.175), kind=kLoop, calls=%fused_computation.29 | loop fusion | flops 1280000 | bytes 3072001 | tf_op jit(solution)/shard_map/dynamic_update_slice | solution.py:196
  (6 shorter events, 0.0 us)
Async XLA Ops:
  29.4 85.4 %collective-permute-start = (bf16[10,200,128]{2,1,0:T(8,128)(2,1)}, bf16[10,200,128]{2,1,0:T(8,128)(2,1)S(1)}, u32[]{:S(2)}, u32[]{:S(2)}) collective-permute-start(bf16[10,200,128]{2,1,0:T(8,128)(2,1)} %get-tuple-element.20), channel_id=1, source_target_pairs={{0,4},{4,0},{8,12},{12,8},{16,20},{20,16},{24,28},{28,24},{1,5},{5... | collective-permute-start | bytes 1536008 | tf_op jit(solution)/shard_map/ppermute | solution.py:188
  46.3 81.1 %collective-permute-start.2 = (bf16[10,200,128]{2,1,0:T(8,128)(2,1)}, bf16[10,200,128]{2,1,0:T(8,128)(2,1)S(1)}, u32[]{:S(2)}, u32[]{:S(2)}) collective-permute-start(bf16[10,200,128]{2,1,0:T(8,128)(2,1)} %get-tuple-element.22), channel_id=1, source_target_pairs={{0,4},{4,0},{8,12},{12,8},{16,20},{20,16},{24,28},{28,24},{1,5},{5... | collective-permute-start | bytes 1536008 | tf_op jit(solution)/shard_map/ppermute | solution.py:188
  62.6 66.4 %collective-permute-start.4 = (bf16[10,200,128]{2,1,0:T(8,128)(2,1)}, bf16[10,200,128]{2,1,0:T(8,128)(2,1)S(1)}, u32[]{:S(2)}, u32[]{:S(2)}) collective-permute-start(bf16[10,200,128]{2,1,0:T(8,128)(2,1)} %get-tuple-element.24), channel_id=1, source_target_pairs={{0,4},{4,0},{8,12},{12,8},{16,20},{20,16},{24,28},{28,24},{1,5},{5... | collective-permute-start | bytes 1536008 | tf_op jit(solution)/shard_map/ppermute | solution.py:188
  79.0 63.9 %collective-permute-start.6 = (bf16[10,200,128]{2,1,0:T(8,128)(2,1)}, bf16[10,200,128]{2,1,0:T(8,128)(2,1)S(1)}, u32[]{:S(2)}, u32[]{:S(2)}) collective-permute-start(bf16[10,200,128]{2,1,0:T(8,128)(2,1)} %get-tuple-element.26), channel_id=1, source_target_pairs={{0,4},{4,0},{8,12},{12,8},{16,20},{20,16},{24,28},{28,24},{1,5},{5... | collective-permute-start | bytes 1536008 | tf_op jit(solution)/shard_map/ppermute | solution.py:188
  95.3 49.2 %collective-permute-start.8 = (bf16[10,200,128]{2,1,0:T(8,128)(2,1)}, bf16[10,200,128]{2,1,0:T(8,128)(2,1)S(1)}, u32[]{:S(2)}, u32[]{:S(2)}) collective-permute-start(bf16[10,200,128]{2,1,0:T(8,128)(2,1)} %get-tuple-element.28), channel_id=1, source_target_pairs={{0,4},{4,0},{8,12},{12,8},{16,20},{20,16},{24,28},{28,24},{1,5},{5... | collective-permute-start | bytes 1536008 | tf_op jit(solution)/shard_map/ppermute | solution.py:188
  99.8 15.1 %copy-start.2 = (bf16[10,200,128]{2,1,0:T(8,128)(2,1)S(1)}, bf16[10,200,128]{2,1,0:T(8,128)(2,1)}, u32[]{:S(2)}) copy-start(bf16[10,200,128]{2,1,0:T(8,128)(2,1)} %get-tuple-element.19) | copy-start | bytes 1536004
  114.8 29.7 %copy-start.3 = (bf16[10,200,128]{2,1,0:T(8,128)(2,1)S(1)}, bf16[10,200,128]{2,1,0:T(8,128)(2,1)}, u32[]{:S(2)}) copy-start(bf16[10,200,128]{2,1,0:T(8,128)(2,1)} %get-tuple-element.27) | copy-start | bytes 1536004
  114.8 36.5 %copy-start = (f32[50,200,128]{2,1,0:T(8,128)S(1)}, f32[50,200,128]{2,1,0:T(8,128)}, u32[]{:S(2)}) copy-start(f32[50,200,128]{2,1,0:T(8,128)} %contract.6) | copy-start | bytes 15360004
  115.0 36.3 %collective-permute-start.1 = (bf16[10,200,128]{2,1,0:T(8,128)(2,1)S(1)}, bf16[10,200,128]{2,1,0:T(8,128)(2,1)S(1)}, u32[]{:S(2)}, u32[]{:S(2)}) collective-permute-start(bf16[10,200,128]{2,1,0:T(8,128)(2,1)S(1)} %fusion.24), channel_id=1, source_target_pairs={{0,8},{4,12},{8,16},{12,20},{16,24},{20,28},{24,0},{28,4},{1,9},{5... | collective-permute-start | bytes 1536008 | tf_op jit(solution)/shard_map/ppermute | solution.py:190
  128.8 33.5 %collective-permute-start.3 = (bf16[10,200,128]{2,1,0:T(8,128)(2,1)S(1)}, bf16[10,200,128]{2,1,0:T(8,128)(2,1)S(1)}, u32[]{:S(2)}, u32[]{:S(2)}) collective-permute-start(bf16[10,200,128]{2,1,0:T(8,128)(2,1)S(1)} %fusion.23), channel_id=1, source_target_pairs={{0,8},{4,12},{8,16},{12,20},{16,24},{20,28},{24,0},{28,4},{1,9},{5... | collective-permute-start | bytes 1536008 | tf_op jit(solution)/shard_map/ppermute | solution.py:190
  130.4 42.8 %collective-permute-start.5 = (bf16[10,200,128]{2,1,0:T(8,128)(2,1)S(1)}, bf16[10,200,128]{2,1,0:T(8,128)(2,1)S(1)}, u32[]{:S(2)}, u32[]{:S(2)}) collective-permute-start(bf16[10,200,128]{2,1,0:T(8,128)(2,1)S(1)} %fusion.22), channel_id=1, source_target_pairs={{0,8},{4,12},{8,16},{12,20},{16,24},{20,28},{24,0},{28,4},{1,9},{5... | collective-permute-start | bytes 1536008 | tf_op jit(solution)/shard_map/ppermute | solution.py:190
  144.3 40.0 %collective-permute-start.7 = (bf16[10,200,128]{2,1,0:T(8,128)(2,1)S(1)}, bf16[10,200,128]{2,1,0:T(8,128)(2,1)S(1)}, u32[]{:S(2)}, u32[]{:S(2)}) collective-permute-start(bf16[10,200,128]{2,1,0:T(8,128)(2,1)S(1)} %fusion.21), channel_id=1, source_target_pairs={{0,8},{4,12},{8,16},{12,20},{16,24},{20,28},{24,0},{28,4},{1,9},{5... | collective-permute-start | bytes 1536008 | tf_op jit(solution)/shard_map/ppermute | solution.py:190
  144.7 50.2 %collective-permute-start.9 = (bf16[10,200,128]{2,1,0:T(8,128)(2,1)S(1)}, bf16[10,200,128]{2,1,0:T(8,128)(2,1)S(1)}, u32[]{:S(2)}, u32[]{:S(2)}) collective-permute-start(bf16[10,200,128]{2,1,0:T(8,128)(2,1)S(1)} %fusion.20), channel_id=1, source_target_pairs={{0,8},{4,12},{8,16},{12,20},{16,24},{20,28},{24,0},{28,4},{1,9},{5... | collective-permute-start | bytes 1536008 | tf_op jit(solution)/shard_map/ppermute | solution.py:190
  184.6 10.3 %copy-start.1 = (f32[50,200,128]{2,1,0:T(8,128)}, f32[50,200,128]{2,1,0:T(8,128)S(1)}, u32[]{:S(2)}) copy-start(f32[50,200,128]{2,1,0:T(8,128)S(1)} %fusion.15) | copy-start | bytes 15360004
where the time goes:
time: 201 us; the launch traced here: 197 us
  Pallas kernels  80.7 us (40%)
  waiting for transfers between devices  48.6 us (24%)
  starting transfers between devices  40 us (20%)
  other arithmetic  15.5 us (8%)
  blocking collectives  8.26 us (4%)
  local copies, waits for them, and re-layouts  3.4 us (2%)
    pallas_call x6, Pallas kernels, contract(): pl.pallas_call(partial(contract_kernel, targets, room), out_shape=outs, i...  79.1 us
    ppermute x5, waiting for transfers between devices, local(): arrived.append(lax.ppermute(send, 'task', ahead))  48.5 us
    ppermute x5, starting transfers between devices, local(): arrived.append(lax.ppermute(send, 'task', ahead))  25.3 us
    ppermute x5, starting transfers between devices, local(): other = lax.ppermute(one, 'task', swap)  14.7 us
    all_gather x1, blocking collectives, local(): coeff_all = lax.all_gather(mo_coeffs, 'occ', axis=1, tiled=True)  8.26 us
    select_n x5, other arithmetic, local(): jnp.where(odd, two, (two.astype(F32) + other.astype(F32)).astype(BF16))  4.55 us
    convert_element_type x6, other arithmetic, contract(): pick = eq(out_rows // GROUP + start, jnp.arange(local_occ)).astype(BF16)  4.14 us
  transfers between devices with their start and end apart: 10, of which 5 were waited for; matrix products, arithmetic and copies ran while one was open for 5% of the time, Pallas kernels for 34%

commit v1 on v0

--- a/solution.py
+++ b/solution.py
@@ -2,6 +2,7 @@
 
 import jax
 import jax.numpy as jnp
+import numpy as np
 from jax import lax
 from jax.experimental import pallas as pl
 from jax.experimental.pallas import tpu as pltpu
@@ -51,10 +52,10 @@
     )(tile_live, batch_target, batch_count)
 
 
-def contract_kernel(targets, room, slots_ref, filled_ref, mu_ref, nu_ref, tiles, *refs):
+def contract_kernel(targets, pieces, room, slots_ref, filled_ref, mu_ref, nu_ref, tiles, *refs):
     coeff_i, coeff_all, pick, own, interleave, unit = refs[:6]
-    outs = refs[6 : 6 + len(targets)]
-    held, turned, quarter, total, landed = refs[6 + len(targets) :]
+    outs = refs[6 : 6 + len(targets) * pieces]
+    held, turned, quarter, total, landed = refs[6 + len(targets) * pieces :]
     _, mu_width, nu_width, kl = tiles.shape
     occ = total.shape[0]
     depth = GROUP * mu_width
@@ -113,7 +114,7 @@
             total[occ - 1] += jnp.dot(right, quarter[occ - 1], preferred_element_type=F32)
         return 1 - slot
 
-    for target, out in zip(targets, outs):
+    for k, target in enumerate(targets):
         groups = lax.div(filled_ref[target] + (GROUP - 1), GROUP)
         total[...] = jnp.zeros_like(total)
 
@@ -123,36 +124,38 @@
                 copy.start()
 
         lax.fori_loop(0, groups, lambda g, slot, t=target, n=groups: visit(t, n, g, slot), jnp.int32(0))
-        out[...] = total[...].astype(out.dtype)
-
-
-def contract(targets, dtype, start, occ, ao_tiles, coeff_i, coeff_all, plan, mu_blocks, nu_blocks):
+        part = occ // pieces
+        for c, out in enumerate(outs[k * pieces : (k + 1) * pieces]):
+            out[...] = total[c * part : (c + 1) * part].astype(out.dtype)
+
+
+def contract(targets, dtype, pieces, ao_tiles, coeff_i, coeff_all, plan, mu_blocks, nu_blocks):
     slots, filled = plan
     count, mu_width, nu_width, kl = ao_tiles.shape
     all_occ = coeff_all.shape[1]
-    local_occ = coeff_i.shape[2]
+    occ = coeff_i.shape[2]
     room = count + GROUP
     depth, width = GROUP * mu_width, GROUP * nu_width
 
-    def eq(rows, columns):
-        return rows[:, None] == columns[None, :]
-
-    out_rows = jnp.arange(occ * GROUP)
-    pick = eq(out_rows // GROUP + start, jnp.arange(local_occ)).astype(BF16)
-    own = eq(out_rows % GROUP, jnp.arange(depth) // mu_width).astype(F32)
-    mixed_rows = jnp.arange(width)
-    interleave = eq(mixed_rows % GROUP * nu_width + mixed_rows // GROUP, mixed_rows).astype(BF16)
-    unit = eq(jnp.arange(all_occ), jnp.arange(all_occ)).astype(BF16)
+    def eq(rows, columns, dtype=BF16):
+        return jnp.asarray(rows[:, None] == columns[None, :], dtype)
+
+    out_rows = np.arange(occ * GROUP)
+    pick = eq(out_rows // GROUP, np.arange(occ))
+    own = eq(out_rows % GROUP, np.arange(depth) // mu_width, F32)
+    mixed_rows = np.arange(width)
+    interleave = eq(mixed_rows % GROUP * nu_width + mixed_rows // GROUP, mixed_rows)
+    unit = eq(np.arange(all_occ), np.arange(all_occ))
     shared = [coeff_i, coeff_all, pick, own, interleave, unit]
     share = occ * len(targets) * max(1, count // GROUP // SPREAD)
-    outs = [jax.ShapeDtypeStruct((occ, all_occ, kl), dtype) for _ in targets]
+    outs = [jax.ShapeDtypeStruct((occ // pieces, all_occ, kl), dtype)] * (len(targets) * pieces)
     return pl.pallas_call(
-        partial(contract_kernel, targets, room),
+        partial(contract_kernel, targets, pieces, room),
         out_shape=outs,
         in_specs=[pl.BlockSpec(memory_space=pltpu.SMEM)] * 4
         + [pl.BlockSpec(memory_space=pl.ANY)]
         + [pl.BlockSpec(memory_space=pltpu.VMEM)] * len(shared),
-        out_specs=[pl.BlockSpec(memory_space=pltpu.VMEM) for _ in targets],
+        out_specs=[pl.BlockSpec(memory_space=pltpu.VMEM)] * len(outs),
         scratch_shapes=[
             pltpu.VMEM((2, GROUP, mu_width, nu_width, kl), BF16),
             pltpu.VMEM((nu_width * depth, kl), F32),
@@ -179,17 +182,16 @@
     ahead = [(t, (t + 2) % tasks) for t in range(tasks)]
     odd = lax.axis_index("task") % 2 == 1
 
-    pieces = next(n for n in range(min(5, local_occ), 0, -1) if local_occ % n == 0)
+    pieces = next(n for n in range(min(10, local_occ), 0, -1) if local_occ % n == 0)
     occ = local_occ // pieces
     work = (ao_tiles, coeff_i, coeff_all, plan, mu_blocks, nu_blocks)
-    swapped, arrived = [], []
-    for c in range(pieces):
-        one, two = contract((1, 2), BF16, c * occ, occ, *work)
-        other = lax.ppermute(one, "task", swap)
+    sums = contract((1, 2), BF16, pieces, *work)
+    swapped = [lax.ppermute(one, "task", swap) for one in sums[:pieces]]
+    arrived = []
+    for two, other in zip(sums[pieces:], swapped):
         send = jnp.where(odd, two, (two.astype(F32) + other.astype(F32)).astype(BF16))
         arrived.append(lax.ppermute(send, "task", ahead))
-        swapped.append(other)
-    (result,) = contract((0,), F32, 0, local_occ, *work)
+    (result,) = contract((0,), F32, 1, *work)
     for c in range(pieces):
         part = lax.slice_in_dim(result, c * occ, (c + 1) * occ, axis=0)
         part = part + (arrived[c].astype(F32) + jnp.where(odd, swapped[c].astype(F32), 0.0))

time: 201 us -> 146 us (0.73); the launches traced: 197 us -> 145 us
  Pallas kernels: 80.7 us -> 37.1 us
  other arithmetic: 15.5 us -> 6.8 us
  starting transfers between devices: 40 us -> 31.9 us
  waiting for transfers between devices: 48.6 us -> 56.7 us
    pallas_call x6 -> x2, Pallas kernels: 79.1 us -> 35.6 us  [contract(): pl.pallas_call(partial(contract_kernel, targets, pieces, room), out_shape...]
    ppermute x5 -> x10, waiting for transfers between devices: 0.01 us -> 26.8 us  [local(): swapped = [lax.ppermute(one, 'task', swap) for one in sums[:pieces]]]
    ppermute x5 -> x10, starting transfers between devices: 25.3 us -> 5.18 us  [local(): arrived.append(lax.ppermute(send, 'task', ahead))]
    ppermute x5 -> x10, waiting for transfers between devices: 48.5 us -> 29.9 us  [local(): arrived.append(lax.ppermute(send, 'task', ahead))]
    ppermute x5 -> x10, starting transfers between devices: 14.7 us -> 26.7 us  [local(): swapped = [lax.ppermute(one, 'task', swap) for one in sums[:pieces]]]
    convert_element_type x10 -> x0, other arithmetic: 7.06 us -> none  [the longest x6 4.14 us: contract(): pick = eq(out_rows // GROUP + start, jnp.arange(local_occ)).astype(BF16)]
    select_n x5 -> x10, other arithmetic: 4.55 us -> 3.05 us  [local(): jnp.where(odd, two, (two.astype(F32) + other.astype(F32)).astype(BF16))]
  transfers between devices with their start and end apart: 10 -> 20, of which waited for: 5 -> 12; matrix products, arithmetic and copies ran while one was open for 5% -> 3% of each run, Pallas kernels for 34% -> 9%
where the time goes in v1:
time: 146 us; the launch traced here: 145 us
  waiting for transfers between devices  56.7 us (39%)
  Pallas kernels  37.1 us (25%)
  starting transfers between devices  31.9 us (22%)
  blocking collectives  8.26 us (6%)
  other arithmetic  6.8 us (5%)
  local copies, waits for them, and re-layouts  3.46 us (2%)
    pallas_call x2, Pallas kernels, contract(): pl.pallas_call(partial(contract_kernel, targets, pieces, room), out_shape...  35.6 us
    ppermute x10, waiting for transfers between devices, local(): arrived.append(lax.ppermute(send, 'task', ahead))  29.9 us
    ppermute x10, waiting for transfers between devices, local(): swapped = [lax.ppermute(one, 'task', swap) for one in sums[:pieces]]  26.8 us
    ppermute x10, starting transfers between devices, local(): swapped = [lax.ppermute(one, 'task', swap) for one in sums[:pieces]]  26.7 us
    all_gather x1, blocking collectives, local(): coeff_all = lax.all_gather(mo_coeffs, 'occ', axis=1, tiled=True)  8.26 us
    ppermute x10, starting transfers between devices, local(): arrived.append(lax.ppermute(send, 'task', ahead))  5.18 us
    dynamic_update_slice x10, other arithmetic, local(): result = lax.dynamic_update_slice_in_dim(result, part, c * occ, axis=0)  3.75 us
    select_n x10, other arithmetic, local(): jnp.where(odd, two, (two.astype(F32) + other.astype(F32)).astype(BF16))  3.05 us
  transfers between devices with their start and end apart: 20, of which 12 were waited for; matrix products, arithmetic and copies ran while one was open for 3% of the time, Pallas kernels for 9%

profile of v1, /device:TPU:4, one launch (start us, length us, event | category | flops | bytes accessed | tf_op | source)
XLA Modules:
  0.0 145.1 jit_solution(13911612578707974176)
XLA Ops:
  0.7 2.0 %copy.20 = f32[1536,50]{1,0:T(8,128)} copy(bf16[1536,50]{0,1:T(8,128)(2,1)} %param.16) | data formatting | bytes 460800 | tf_op jit(solution)/shard_map/reshape | solution.py:179
  2.7 8.3 %all-gather = bf16[4,50,1536]{2,1,0:T(8,128)(2,1)S(1)} all-gather(bf16[1,50,1536]{2,1,0:T(8,128)(2,1)} %bitcast.9), channel_id=1, replica_groups=mesh['task'=8,'occ'=4] {'occ'}, dimensions={0}, use_global_device_ids=true | all-gather | bytes 768000 | tf_op jit(solution)/shard_map/all_gather | solution.py:178
  10.9 0.2 reshape.10
  11.1 1.2 copy.21
  12.3 1.5 %plan.1 = (s32[504]{0:T(512)}, s32[3]{0:T(128)}) custom-call(s32[160]{0:T(256)} %live_ref.1, s32[20]{0:T(128)} %target_ref.1, s32[1]{0:T(128)S(6)} %copy.32.count_ref), custom_call_target="tpu_custom_call" | custom-call | tf_op jit(solution)/shard_map/plan/pallas_call | solution.py:43
  13.8 23.1 %contract.3 = (bf16[5,200,128]{2,1,0:T(8,128)(2,1)}, bf16[5,200,128]{2,1,0:T(8,128)(2,1)}, bf16[5,200,128]{2,1,0:T(8,128)(2,1)}, bf16[5,200,128]{2,1,0:T(8,128)(...) custom-call(s32[504]{0:T(512)} %get-tuple-element.27.slots_ref, ...), custom_call_target="tpu_custom_call" | custom-call | flops 15728640000 | bytes 15360000 | tf_op jit(solution)/shard_map/contract/pallas_call | solution.py:152
  36.9 12.9 %collective-permute-start = (bf16[5,200,128]{2,1,0:T(8,128)(2,1)}, bf16[5,200,128]{2,1,0:T(8,128)(2,1)S(1)}, u32[]{:S(2)}, u32[]{:S(2)}) collective-permute-start(bf16[5,200,128]{2,1,0:T(8,128)(2,1)} %get-tuple-element.30), channel_id=1, source_target_pairs={{0,4},{4,0},{8,12},{12,8},{16,20},{20,16},{24,28},{28,24},{1,5},{5... | collective-permute-start | bytes 768008 | tf_op jit(solution)/shard_map/ppermute | solution.py:189
  49.9 0.1 collective-permute-start.2
  49.9 1.9 %collective-permute-start.4 = (bf16[5,200,128]{2,1,0:T(8,128)(2,1)}, bf16[5,200,128]{2,1,0:T(8,128)(2,1)S(1)}, u32[]{:S(2)}, u32[]{:S(2)}) collective-permute-start(bf16[5,200,128]{2,1,0:T(8,128)(2,1)} %get-tuple-element.34), channel_id=1, source_target_pairs={{0,4},{4,0},{8,12},{12,8},{16,20},{20,16},{24,28},{28,24},{1,5},{5... | collective-permute-start | bytes 768008 | tf_op jit(solution)/shard_map/ppermute | solution.py:189
  51.9 0.1 collective-permute-start.6
  52.0 2.0 %collective-permute-start.8 = (bf16[5,200,128]{2,1,0:T(8,128)(2,1)}, bf16[5,200,128]{2,1,0:T(8,128)(2,1)S(1)}, u32[]{:S(2)}, u32[]{:S(2)}) collective-permute-start(bf16[5,200,128]{2,1,0:T(8,128)(2,1)} %get-tuple-element.38), channel_id=1, source_target_pairs={{0,4},{4,0},{8,12},{12,8},{16,20},{20,16},{24,28},{28,24},{1,5},{5... | collective-permute-start | bytes 768008 | tf_op jit(solution)/shard_map/ppermute | solution.py:189
  54.0 12.5 %contract.2 = f32[50,200,128]{2,1,0:T(8,128)} custom-call(s32[504]{0:T(512)} %get-tuple-element.27.slots_ref, s32[3]{0:T(128)} %get-tuple-element.28.filled_ref, s32[160]{0:T(256)} %mu_ref.3, s32[160]{0:T(256)} %nu_ref.3, bf16[160,8,32,128]{3,2,1,0:T(8,128)(2,1)} %tiles.3, f32[192,8,50]{2,1,0:T(8,128)} %bitcast.6, bf16[1536,200]{1,0:T(8,128)(2,1)} %bitcast.8, ...), custom_call_target="tpu_custom_call" | custom-call | flops 7864320000 | bytes 7680000 | tf_op jit(solution)/shard_map/contract/pallas_call | solution.py:152
  66.6 0.0 copy-start
  66.6 0.0 collective-permute-done
  66.6 5.2 %collective-permute-start.10 = (bf16[5,200,128]{2,1,0:T(8,128)(2,1)}, bf16[5,200,128]{2,1,0:T(8,128)(2,1)S(1)}, u32[]{:S(2)}, u32[]{:S(2)}) collective-permute-start(bf16[5,200,128]{2,1,0:T(8,128)(2,1)} %get-tuple-element.40), channel_id=1, source_target_pairs={{0,4},{4,0},{8,12},{12,8},{16,20},{20,16},{24,28},{28,24},{1,5},{5... | collective-permute-start | bytes 768008 | tf_op jit(solution)/shard_map/ppermute | solution.py:189
  71.8 1.2 fusion.49
  73.0 0.0 collective-permute-done.2
  73.0 0.3 collective-permute-start.12
  73.3 1.2 fusion.48
  74.5 0.0 collective-permute-done.4
  74.5 1.9 %collective-permute-start.14 = (bf16[5,200,128]{2,1,0:T(8,128)(2,1)}, bf16[5,200,128]{2,1,0:T(8,128)(2,1)S(1)}, u32[]{:S(2)}, u32[]{:S(2)}) collective-permute-start(bf16[5,200,128]{2,1,0:T(8,128)(2,1)} %get-tuple-element.44), channel_id=1, source_target_pairs={{0,4},{4,0},{8,12},{12,8},{16,20},{20,16},{24,28},{28,24},{1,5},{5... | collective-permute-start | bytes 768008 | tf_op jit(solution)/shard_map/ppermute | solution.py:189
  76.4 0.1 fusion.47
  76.5 0.0 collective-permute-done.6
  76.5 0.3 collective-permute-start.16
  76.7 0.1 fusion.46
  76.8 2.2 %collective-permute-done.8 = bf16[5,200,128]{2,1,0:T(8,128)(2,1)S(1)} collective-permute-done((bf16[5,200,128]{2,1,0:T(8,128)(2,1)}, bf16[5,200,128]{2,1,0:T(8,128)(2,1)S(1)}, u32[]{:S(2)}, u32[]{:S(2)}) %collective-permute-start.8) | collective-permute-done | bytes 256032 | tf_op jit(solution)/shard_map/ppermute | solution.py:189
  79.0 2.0 %collective-permute-start.18 = (bf16[5,200,128]{2,1,0:T(8,128)(2,1)}, bf16[5,200,128]{2,1,0:T(8,128)(2,1)S(1)}, u32[]{:S(2)}, u32[]{:S(2)}) collective-permute-start(bf16[5,200,128]{2,1,0:T(8,128)(2,1)} %get-tuple-element.48), channel_id=1, source_target_pairs={{0,4},{4,0},{8,12},{12,8},{16,20},{20,16},{24,28},{28,24},{1,5},{5... | collective-permute-start | bytes 768008 | tf_op jit(solution)/shard_map/ppermute | solution.py:189
  81.1 0.1 fusion.45
  81.1 3.4 %collective-permute-done.10 = bf16[5,200,128]{2,1,0:T(8,128)(2,1)S(1)} collective-permute-done((bf16[5,200,128]{2,1,0:T(8,128)(2,1)}, bf16[5,200,128]{2,1,0:T(8,128)(2,1)S(1)}, u32[]{:S(2)}, u32[]{:S(2)}) %collective-permute-start.10) | collective-permute-done | bytes 256032 | tf_op jit(solution)/shard_map/ppermute | solution.py:189
  84.5 0.0 collective-permute-start.1
  84.5 0.1 fusion.44
  84.6 5.4 %collective-permute-done.12 = bf16[5,200,128]{2,1,0:T(8,128)(2,1)S(1)} collective-permute-done((bf16[5,200,128]{2,1,0:T(8,128)(2,1)}, bf16[5,200,128]{2,1,0:T(8,128)(2,1)S(1)}, u32[]{:S(2)}, u32[]{:S(2)}) %collective-permute-start.12) | collective-permute-done | bytes 256032 | tf_op jit(solution)/shard_map/ppermute | solution.py:189
  90.0 0.0 collective-permute-start.3
  90.0 0.1 fusion.43
  90.1 5.4 %collective-permute-done.14 = bf16[5,200,128]{2,1,0:T(8,128)(2,1)S(1)} collective-permute-done((bf16[5,200,128]{2,1,0:T(8,128)(2,1)}, bf16[5,200,128]{2,1,0:T(8,128)(2,1)S(1)}, u32[]{:S(2)}, u32[]{:S(2)}) %collective-permute-start.14) | collective-permute-done | bytes 256032 | tf_op jit(solution)/shard_map/ppermute | solution.py:189
  95.5 0.1 fusion.42
  95.6 5.4 %collective-permute-done.16 = bf16[5,200,128]{2,1,0:T(8,128)(2,1)S(1)} collective-permute-done((bf16[5,200,128]{2,1,0:T(8,128)(2,1)}, bf16[5,200,128]{2,1,0:T(8,128)(2,1)S(1)}, u32[]{:S(2)}, u32[]{:S(2)}) %collective-permute-start.16) | collective-permute-done | bytes 256032 | tf_op jit(solution)/shard_map/ppermute | solution.py:189
  101.0 0.0 collective-permute-start.7
  101.0 0.1 fusion.41
  101.1 5.1 %collective-permute-done.18 = bf16[5,200,128]{2,1,0:T(8,128)(2,1)S(1)} collective-permute-done((bf16[5,200,128]{2,1,0:T(8,128)(2,1)}, bf16[5,200,128]{2,1,0:T(8,128)(2,1)S(1)}, u32[]{:S(2)}, u32[]{:S(2)}) %collective-permute-start.18) | collective-permute-done | bytes 256032 | tf_op jit(solution)/shard_map/ppermute | solution.py:189
  106.1 0.0 collective-permute-start.9
  106.1 0.1 fusion.40
  106.2 0.1 collective-permute-start.11
  106.3 0.2 fusion.3
  106.5 0.0 collective-permute-done.3
  106.5 0.2 collective-permute-start.13
  106.7 0.2 fusion.7
  106.9 4.9 %collective-permute-start.15 = (bf16[5,200,128]{2,1,0:T(8,128)(2,1)S(1)}, bf16[5,200,128]{2,1,0:T(8,128)(2,1)S(1)}, u32[]{:S(2)}, u32[]{:S(2)}) collective-permute-start(bf16[5,200,128]{2,1,0:T(8,128)(2,1)S(1)} %fusion.42), channel_id=1, source_target_pairs={{0,8},{4,12},{8,16},{12,20},{16,24},{20,28},{24,0},{28,4},{1,9},{5... | collective-permute-start | bytes 768008 | tf_op jit(solution)/shard_map/ppermute | solution.py:193
  111.8 0.2 fusion.11
  112.0 0.1 collective-permute-start.17
  112.1 0.2 fusion.15
  112.3 4.7 %collective-permute-done.9 = bf16[5,200,128]{2,1,0:T(8,128)(2,1)S(1)} collective-permute-done((bf16[5,200,128]{2,1,0:T(8,128)(2,1)S(1)}, bf16[5,200,128]{2,1,0:T(8,128)(2,1)S(1)}, u32[]{:S(2)}, u32[]{:S(2)}) %collective-permute-start.9) | collective-permute-done | bytes 256032 | tf_op jit(solution)/shard_map/ppermute | solution.py:193
  117.0 0.2 fusion.19
  117.2 5.3 %collective-permute-done.11 = bf16[5,200,128]{2,1,0:T(8,128)(2,1)S(1)} collective-permute-done((bf16[5,200,128]{2,1,0:T(8,128)(2,1)S(1)}, bf16[5,200,128]{2,1,0:T(8,128)(2,1)S(1)}, u32[]{:S(2)}, u32[]{:S(2)}) %collective-permute-start.11) | collective-permute-done | bytes 256032 | tf_op jit(solution)/shard_map/ppermute | solution.py:193
  122.5 0.2 fusion.23
  122.7 5.3 %collective-permute-done.13 = bf16[5,200,128]{2,1,0:T(8,128)(2,1)S(1)} collective-permute-done((bf16[5,200,128]{2,1,0:T(8,128)(2,1)S(1)}, bf16[5,200,128]{2,1,0:T(8,128)(2,1)S(1)}, u32[]{:S(2)}, u32[]{:S(2)}) %collective-permute-start.13) | collective-permute-done | bytes 256032 | tf_op jit(solution)/shard_map/ppermute | solution.py:193
  127.9 0.2 fusion.27
  128.1 5.3 %collective-permute-done.15 = bf16[5,200,128]{2,1,0:T(8,128)(2,1)S(1)} collective-permute-done((bf16[5,200,128]{2,1,0:T(8,128)(2,1)S(1)}, bf16[5,200,128]{2,1,0:T(8,128)(2,1)S(1)}, u32[]{:S(2)}, u32[]{:S(2)}) %collective-permute-start.15) | collective-permute-done | bytes 256032 | tf_op jit(solution)/shard_map/ppermute | solution.py:193
  133.4 0.2 fusion.31
  133.6 5.3 %collective-permute-done.17 = bf16[5,200,128]{2,1,0:T(8,128)(2,1)S(1)} collective-permute-done((bf16[5,200,128]{2,1,0:T(8,128)(2,1)S(1)}, bf16[5,200,128]{2,1,0:T(8,128)(2,1)S(1)}, u32[]{:S(2)}, u32[]{:S(2)}) %collective-permute-start.17) | collective-permute-done | bytes 256032 | tf_op jit(solution)/shard_map/ppermute | solution.py:193
  138.9 0.2 fusion.35
  139.1 0.0 copy-start.1
  139.1 4.1 %collective-permute-done.19 = bf16[5,200,128]{2,1,0:T(8,128)(2,1)S(1)} collective-permute-done((bf16[5,200,128]{2,1,0:T(8,128)(2,1)S(1)}, bf16[5,200,128]{2,1,0:T(8,128)(2,1)S(1)}, u32[]{:S(2)}, u32[]{:S(2)}) %collective-permute-start.19) | collective-permute-done | bytes 256032 | tf_op jit(solution)/shard_map/ppermute | solution.py:193
  143.2 1.9 %fusion.39 = f32[50,200,128]{2,1,0:T(8,128)} fusion(f32[50,200,128]{2,1,0:T(8,128)} %copy-done.1, bf16[5,200,128]{2,1,0:T(8,128)(2,1)S(1)} %collective-permute-done.18, bf16[5,200,128]{2,1,0:T(8,128)(2,1)S(1)} %collective-permute-done.19, pred[]{:T(512)S(6)} %eq.5), kind=kLoop, calls=%fused_computation.59 | loop fusion | flops 640000 | bytes 1536001 | tf_op jit(solution)/shard_map/dynamic_update_slice | solution.py:198
  (23 shorter events, 0.0 us)
Async XLA Ops:
  36.9 29.6 %collective-permute-start = (bf16[5,200,128]{2,1,0:T(8,128)(2,1)}, bf16[5,200,128]{2,1,0:T(8,128)(2,1)S(1)}, u32[]{:S(2)}, u32[]{:S(2)}) collective-permute-start(bf16[5,200,128]{2,1,0:T(8,128)(2,1)} %get-tuple-element.30), channel_id=1, source_target_pairs={{0,4},{4,0},{8,12},{12,8},{16,20},{20,16},{24,28},{28,24},{1,5},{5... | collective-permute-start | bytes 768008 | tf_op jit(solution)/shard_map/ppermute | solution.py:189
  49.9 23.2 %collective-permute-start.2 = (bf16[5,200,128]{2,1,0:T(8,128)(2,1)}, bf16[5,200,128]{2,1,0:T(8,128)(2,1)S(1)}, u32[]{:S(2)}, u32[]{:S(2)}) collective-permute-start(bf16[5,200,128]{2,1,0:T(8,128)(2,1)} %get-tuple-element.32), channel_id=1, source_target_pairs={{0,4},{4,0},{8,12},{12,8},{16,20},{20,16},{24,28},{28,24},{1,5},{5... | collective-permute-start | bytes 768008 | tf_op jit(solution)/shard_map/ppermute | solution.py:189
  49.9 24.5 %collective-permute-start.4 = (bf16[5,200,128]{2,1,0:T(8,128)(2,1)}, bf16[5,200,128]{2,1,0:T(8,128)(2,1)S(1)}, u32[]{:S(2)}, u32[]{:S(2)}) collective-permute-start(bf16[5,200,128]{2,1,0:T(8,128)(2,1)} %get-tuple-element.34), channel_id=1, source_target_pairs={{0,4},{4,0},{8,12},{12,8},{16,20},{20,16},{24,28},{28,24},{1,5},{5... | collective-permute-start | bytes 768008 | tf_op jit(solution)/shard_map/ppermute | solution.py:189
  51.9 24.6 %collective-permute-start.6 = (bf16[5,200,128]{2,1,0:T(8,128)(2,1)}, bf16[5,200,128]{2,1,0:T(8,128)(2,1)S(1)}, u32[]{:S(2)}, u32[]{:S(2)}) collective-permute-start(bf16[5,200,128]{2,1,0:T(8,128)(2,1)} %get-tuple-element.36), channel_id=1, source_target_pairs={{0,4},{4,0},{8,12},{12,8},{16,20},{20,16},{24,28},{28,24},{1,5},{5... | collective-permute-start | bytes 768008 | tf_op jit(solution)/shard_map/ppermute | solution.py:189
  52.0 24.4 %copy-start.9 = (bf16[5,200,128]{2,1,0:T(8,128)(2,1)S(1)}, bf16[5,200,128]{2,1,0:T(8,128)(2,1)}, u32[]{:S(2)}) copy-start(bf16[5,200,128]{2,1,0:T(8,128)(2,1)} %get-tuple-element.33) | copy-start | bytes 768004
  52.0 24.8 %copy-start.8 = (bf16[5,200,128]{2,1,0:T(8,128)(2,1)S(1)}, bf16[5,200,128]{2,1,0:T(8,128)(2,1)}, u32[]{:S(2)}) copy-start(bf16[5,200,128]{2,1,0:T(8,128)(2,1)} %get-tuple-element.35) | copy-start | bytes 768004
  52.0 29.1 %copy-start.7 = (bf16[5,200,128]{2,1,0:T(8,128)(2,1)S(1)}, bf16[5,200,128]{2,1,0:T(8,128)(2,1)}, u32[]{:S(2)}) copy-start(bf16[5,200,128]{2,1,0:T(8,128)(2,1)} %get-tuple-element.37) | copy-start | bytes 768004
  52.0 32.6 %copy-start.6 = (bf16[5,200,128]{2,1,0:T(8,128)(2,1)S(1)}, bf16[5,200,128]{2,1,0:T(8,128)(2,1)}, u32[]{:S(2)}) copy-start(bf16[5,200,128]{2,1,0:T(8,128)(2,1)} %get-tuple-element.39) | copy-start | bytes 768004
  52.0 38.0 %copy-start.5 = (bf16[5,200,128]{2,1,0:T(8,128)(2,1)S(1)}, bf16[5,200,128]{2,1,0:T(8,128)(2,1)}, u32[]{:S(2)}) copy-start(bf16[5,200,128]{2,1,0:T(8,128)(2,1)} %get-tuple-element.41) | copy-start | bytes 768004
  52.0 27.1 %collective-permute-start.8 = (bf16[5,200,128]{2,1,0:T(8,128)(2,1)}, bf16[5,200,128]{2,1,0:T(8,128)(2,1)S(1)}, u32[]{:S(2)}, u32[]{:S(2)}) collective-permute-start(bf16[5,200,128]{2,1,0:T(8,128)(2,1)} %get-tuple-element.38), channel_id=1, source_target_pairs={{0,4},{4,0},{8,12},{12,8},{16,20},{20,16},{24,28},{28,24},{1,5},{5... | collective-permute-start | bytes 768008 | tf_op jit(solution)/shard_map/ppermute | solution.py:189
  66.5 29.0 %copy-start.4 = (bf16[5,200,128]{2,1,0:T(8,128)(2,1)S(1)}, bf16[5,200,128]{2,1,0:T(8,128)(2,1)}, u32[]{:S(2)}) copy-start(bf16[5,200,128]{2,1,0:T(8,128)(2,1)} %get-tuple-element.43) | copy-start | bytes 768004
  66.5 34.4 %copy-start.3 = (bf16[5,200,128]{2,1,0:T(8,128)(2,1)S(1)}, bf16[5,200,128]{2,1,0:T(8,128)(2,1)}, u32[]{:S(2)}) copy-start(bf16[5,200,128]{2,1,0:T(8,128)(2,1)} %get-tuple-element.45) | copy-start | bytes 768004
  66.5 39.6 %copy-start.2 = (bf16[5,200,128]{2,1,0:T(8,128)(2,1)S(1)}, bf16[5,200,128]{2,1,0:T(8,128)(2,1)}, u32[]{:S(2)}) copy-start(bf16[5,200,128]{2,1,0:T(8,128)(2,1)} %get-tuple-element.47) | copy-start | bytes 768004
  66.6 39.7 %copy-start = (f32[50,200,128]{2,1,0:T(8,128)S(1)}, f32[50,200,128]{2,1,0:T(8,128)}, u32[]{:S(2)}) copy-start(f32[50,200,128]{2,1,0:T(8,128)} %contract.2) | copy-start | bytes 15360004
  66.6 17.9 %collective-permute-start.10 = (bf16[5,200,128]{2,1,0:T(8,128)(2,1)}, bf16[5,200,128]{2,1,0:T(8,128)(2,1)S(1)}, u32[]{:S(2)}, u32[]{:S(2)}) collective-permute-start(bf16[5,200,128]{2,1,0:T(8,128)(2,1)} %get-tuple-element.40), channel_id=1, source_target_pairs={{0,4},{4,0},{8,12},{12,8},{16,20},{20,16},{24,28},{28,24},{1,5},{5... | collective-permute-start | bytes 768008 | tf_op jit(solution)/shard_map/ppermute | solution.py:189
  73.0 17.0 %collective-permute-start.12 = (bf16[5,200,128]{2,1,0:T(8,128)(2,1)}, bf16[5,200,128]{2,1,0:T(8,128)(2,1)S(1)}, u32[]{:S(2)}, u32[]{:S(2)}) collective-permute-start(bf16[5,200,128]{2,1,0:T(8,128)(2,1)} %get-tuple-element.42), channel_id=1, source_target_pairs={{0,4},{4,0},{8,12},{12,8},{16,20},{20,16},{24,28},{28,24},{1,5},{5... | collective-permute-start | bytes 768008 | tf_op jit(solution)/shard_map/ppermute | solution.py:189
  74.5 21.0 %collective-permute-start.14 = (bf16[5,200,128]{2,1,0:T(8,128)(2,1)}, bf16[5,200,128]{2,1,0:T(8,128)(2,1)S(1)}, u32[]{:S(2)}, u32[]{:S(2)}) collective-permute-start(bf16[5,200,128]{2,1,0:T(8,128)(2,1)} %get-tuple-element.44), channel_id=1, source_target_pairs={{0,4},{4,0},{8,12},{12,8},{16,20},{20,16},{24,28},{28,24},{1,5},{5... | collective-permute-start | bytes 768008 | tf_op jit(solution)/shard_map/ppermute | solution.py:189
  76.5 24.5 %collective-permute-start.16 = (bf16[5,200,128]{2,1,0:T(8,128)(2,1)}, bf16[5,200,128]{2,1,0:T(8,128)(2,1)S(1)}, u32[]{:S(2)}, u32[]{:S(2)}) collective-permute-start(bf16[5,200,128]{2,1,0:T(8,128)(2,1)} %get-tuple-element.46), channel_id=1, source_target_pairs={{0,4},{4,0},{8,12},{12,8},{16,20},{20,16},{24,28},{28,24},{1,5},{5... | collective-permute-start | bytes 768008 | tf_op jit(solution)/shard_map/ppermute | solution.py:189
  79.0 27.1 %collective-permute-start.18 = (bf16[5,200,128]{2,1,0:T(8,128)(2,1)}, bf16[5,200,128]{2,1,0:T(8,128)(2,1)S(1)}, u32[]{:S(2)}, u32[]{:S(2)}) collective-permute-start(bf16[5,200,128]{2,1,0:T(8,128)(2,1)} %get-tuple-element.48), channel_id=1, source_target_pairs={{0,4},{4,0},{8,12},{12,8},{16,20},{20,16},{24,28},{28,24},{1,5},{5... | collective-permute-start | bytes 768008 | tf_op jit(solution)/shard_map/ppermute | solution.py:189
  84.5 21.7 %collective-permute-start.1 = (bf16[5,200,128]{2,1,0:T(8,128)(2,1)S(1)}, bf16[5,200,128]{2,1,0:T(8,128)(2,1)S(1)}, u32[]{:S(2)}, u32[]{:S(2)}) collective-permute-start(bf16[5,200,128]{2,1,0:T(8,128)(2,1)S(1)} %fusion.49), channel_id=1, source_target_pairs={{0,8},{4,12},{8,16},{12,20},{16,24},{20,28},{24,0},{28,4},{1,9},{5... | collective-permute-start | bytes 768008 | tf_op jit(solution)/shard_map/ppermute | solution.py:193
  90.0 16.5 %collective-permute-start.3 = (bf16[5,200,128]{2,1,0:T(8,128)(2,1)S(1)}, bf16[5,200,128]{2,1,0:T(8,128)(2,1)S(1)}, u32[]{:S(2)}, u32[]{:S(2)}) collective-permute-start(bf16[5,200,128]{2,1,0:T(8,128)(2,1)S(1)} %fusion.48), channel_id=1, source_target_pairs={{0,8},{4,12},{8,16},{12,20},{16,24},{20,28},{24,0},{28,4},{1,9},{5... | collective-permute-start | bytes 768008 | tf_op jit(solution)/shard_map/ppermute | solution.py:193
  95.5 11.4 %collective-permute-start.5 = (bf16[5,200,128]{2,1,0:T(8,128)(2,1)S(1)}, bf16[5,200,128]{2,1,0:T(8,128)(2,1)S(1)}, u32[]{:S(2)}, u32[]{:S(2)}) collective-permute-start(bf16[5,200,128]{2,1,0:T(8,128)(2,1)S(1)} %fusion.47), channel_id=1, source_target_pairs={{0,8},{4,12},{8,16},{12,20},{16,24},{20,28},{24,0},{28,4},{1,9},{5... | collective-permute-start | bytes 768008 | tf_op jit(solution)/shard_map/ppermute | solution.py:193
  101.0 11.0 %collective-permute-start.7 = (bf16[5,200,128]{2,1,0:T(8,128)(2,1)S(1)}, bf16[5,200,128]{2,1,0:T(8,128)(2,1)S(1)}, u32[]{:S(2)}, u32[]{:S(2)}) collective-permute-start(bf16[5,200,128]{2,1,0:T(8,128)(2,1)S(1)} %fusion.46), channel_id=1, source_target_pairs={{0,8},{4,12},{8,16},{12,20},{16,24},{20,28},{24,0},{28,4},{1,9},{5... | collective-permute-start | bytes 768008 | tf_op jit(solution)/shard_map/ppermute | solution.py:193
  106.1 10.8 %collective-permute-start.9 = (bf16[5,200,128]{2,1,0:T(8,128)(2,1)S(1)}, bf16[5,200,128]{2,1,0:T(8,128)(2,1)S(1)}, u32[]{:S(2)}, u32[]{:S(2)}) collective-permute-start(bf16[5,200,128]{2,1,0:T(8,128)(2,1)S(1)} %fusion.45), channel_id=1, source_target_pairs={{0,8},{4,12},{8,16},{12,20},{16,24},{20,28},{24,0},{28,4},{1,9},{5... | collective-permute-start | bytes 768008 | tf_op jit(solution)/shard_map/ppermute | solution.py:193
  106.2 16.2 %collective-permute-start.11 = (bf16[5,200,128]{2,1,0:T(8,128)(2,1)S(1)}, bf16[5,200,128]{2,1,0:T(8,128)(2,1)S(1)}, u32[]{:S(2)}, u32[]{:S(2)}) collective-permute-start(bf16[5,200,128]{2,1,0:T(8,128)(2,1)S(1)} %fusion.44), channel_id=1, source_target_pairs={{0,8},{4,12},{8,16},{12,20},{16,24},{20,28},{24,0},{28,4},{1,9},{5... | collective-permute-start | bytes 768008 | tf_op jit(solution)/shard_map/ppermute | solution.py:193
  106.5 21.4 %collective-permute-start.13 = (bf16[5,200,128]{2,1,0:T(8,128)(2,1)S(1)}, bf16[5,200,128]{2,1,0:T(8,128)(2,1)S(1)}, u32[]{:S(2)}, u32[]{:S(2)}) collective-permute-start(bf16[5,200,128]{2,1,0:T(8,128)(2,1)S(1)} %fusion.43), channel_id=1, source_target_pairs={{0,8},{4,12},{8,16},{12,20},{16,24},{20,28},{24,0},{28,4},{1,9},{5... | collective-permute-start | bytes 768008 | tf_op jit(solution)/shard_map/ppermute | solution.py:193
  106.9 26.5 %collective-permute-start.15 = (bf16[5,200,128]{2,1,0:T(8,128)(2,1)S(1)}, bf16[5,200,128]{2,1,0:T(8,128)(2,1)S(1)}, u32[]{:S(2)}, u32[]{:S(2)}) collective-permute-start(bf16[5,200,128]{2,1,0:T(8,128)(2,1)S(1)} %fusion.42), channel_id=1, source_target_pairs={{0,8},{4,12},{8,16},{12,20},{16,24},{20,28},{24,0},{28,4},{1,9},{5... | collective-permute-start | bytes 768008 | tf_op jit(solution)/shard_map/ppermute | solution.py:193
  112.0 26.9 %collective-permute-start.17 = (bf16[5,200,128]{2,1,0:T(8,128)(2,1)S(1)}, bf16[5,200,128]{2,1,0:T(8,128)(2,1)S(1)}, u32[]{:S(2)}, u32[]{:S(2)}) collective-permute-start(bf16[5,200,128]{2,1,0:T(8,128)(2,1)S(1)} %fusion.41), channel_id=1, source_target_pairs={{0,8},{4,12},{8,16},{12,20},{16,24},{20,28},{24,0},{28,4},{1,9},{5... | collective-permute-start | bytes 768008 | tf_op jit(solution)/shard_map/ppermute | solution.py:193
  117.0 26.2 %collective-permute-start.19 = (bf16[5,200,128]{2,1,0:T(8,128)(2,1)S(1)}, bf16[5,200,128]{2,1,0:T(8,128)(2,1)S(1)}, u32[]{:S(2)}, u32[]{:S(2)}) collective-permute-start(bf16[5,200,128]{2,1,0:T(8,128)(2,1)S(1)} %fusion.40), channel_id=1, source_target_pairs={{0,8},{4,12},{8,16},{12,20},{16,24},{20,28},{24,0},{28,4},{1,9},{5... | collective-permute-start | bytes 768008 | tf_op jit(solution)/shard_map/ppermute | solution.py:193
  139.1 4.1 %copy-start.1 = (f32[50,200,128]{2,1,0:T(8,128)}, f32[50,200,128]{2,1,0:T(8,128)S(1)}, u32[]{:S(2)}) copy-start(f32[50,200,128]{2,1,0:T(8,128)S(1)} %fusion.35) | copy-start | bytes 15360004
